TPU v7x, 32 devices: a whole 2x2x4 slice. The times are simulated.
32 devices in a mesh: fsdp: 8 (over y, x, core), dp: 4 (over z).
Axes of the slice: x: 2, y: 2, z: 4, core: 2. Of those that a mesh axis runs over, the one named last changes fastest.
Arguments:
- tokens: bfloat16 [4096, 1536], P(('fsdp', 'dp')), may hold values from -6 to 6
- lengths: int32 [32, 4], P('fsdp'), may hold values from 1 to 64, 128 in all within a row
- cotangent: bfloat16 [4096, 1536], P(('fsdp', 'dp')), may hold values from -6 to 6
- attn_gain: bfloat16 [1, 1536], P(None, 'fsdp'), may hold values from 0.5 to 1.5
- w_query: bfloat16 [1, 1536, 1536], P(None, 'fsdp', 'dp'), may hold values from -0.15625 to 0.15625
- w_key: bfloat16 [1, 1536, 768], P(None, 'fsdp', 'dp'), may hold values from -0.15625 to 0.15625
- w_value: bfloat16 [1, 1536, 768], P(None, 'fsdp', 'dp'), may hold values from -0.15625 to 0.15625
- w_out: bfloat16 [1, 1536, 1536], P(None, 'dp', 'fsdp'), may hold values from -0.875 to 0.875
- mlp_gain: bfloat16 [1, 1536], P(None, 'fsdp'), may hold values from 0.5 to 1.5
- w_gate: bfloat16 [1, 1536, 4096], P(None, 'fsdp', 'dp'), may hold values from -0.15625 to 0.15625
- w_up: bfloat16 [1, 1536, 4096], P(None, 'fsdp', 'dp'), may hold values from -0.15625 to 0.15625
- w_down: bfloat16 [1, 4096, 1536], P(None, 'dp', 'fsdp'), may hold values from -0.09375 to 0.09375
Outputs:
- output: bfloat16 [4096, 1536], P(('fsdp', 'dp'))
- grad_tokens: float32 [4096, 1536], P(('fsdp', 'dp'))
- grad_attn_gain: float32 [1, 1536], P(None, 'fsdp')
- grad_w_query: float32 [1, 1536, 1536], P(None, 'fsdp', 'dp')
- grad_w_key: float32 [1, 1536, 768], P(None, 'fsdp', 'dp')
- grad_w_value: float32 [1, 1536, 768], P(None, 'fsdp', 'dp')
- grad_w_out: float32 [1, 1536, 1536], P(None, 'dp', 'fsdp')
- grad_mlp_gain: float32 [1, 1536], P(None, 'fsdp')
- grad_w_gate: float32 [1, 1536, 4096], P(None, 'fsdp', 'dp')
- grad_w_up: float32 [1, 1536, 4096], P(None, 'fsdp', 'dp')
- grad_w_down: float32 [1, 4096, 1536], P(None, 'dp', 'fsdp')
Inputs may be any that keep to these rules, and one draw needn't show every extreme that they name: `lengths`: each row sums to 128 and its largest entry is 64.
All inputs are finite; a program needn't handle non-finite values.
Results may differ from a plain program's by a relative error of at most 0.019.
Values may be sent and summed in bfloat16 or wider, within the bound.
A program may use at most 320 MiB of HBM per device.

v0:
```python
from functools import partial
import jax
import jax.numpy as jnp
from jax import lax
from jax.sharding import PartitionSpec as P

HD = 96
LAYERS = 1
EPSILON = 1e-05
ROPE_BASE = 100000.0
NEG_FILL = -1e30


def layout(seq_lengths, rows_here):
    seg_ends = jnp.cumsum(seq_lengths)
    seg_starts = seg_ends - seq_lengths
    positions = jnp.arange(rows_here, dtype=jnp.int32)
    segment = jnp.sum((positions[:, None] >= seg_ends[None, :]).astype(jnp.int32), axis=1)
    member = segment[:, None] == jnp.arange(seq_lengths.shape[0], dtype=jnp.int32)[None, :]
    offset = jnp.sum(jnp.where(member, seg_starts[None, :], 0), axis=1)
    where_in = positions - offset
    allowed = (segment[:, None] == segment[None, :]) & (positions[None, :] <= positions[:, None])
    half_dim = HD // 2
    frequency = ROPE_BASE ** (-jnp.arange(half_dim, dtype=jnp.float32) / half_dim)
    angles = where_in.astype(jnp.float32)[:, None] * frequency[None, :]
    return (allowed, jnp.cos(angles), jnp.sin(angles))


def rotate(values, cosine, sine_tab, sign_flip):
    half_dim = values.shape[-1] // 2
    front_half = values[..., :half_dim]
    back_half = values[..., half_dim:]
    cos_part = cosine[:, None, :]
    sin_part = sign_flip * sine_tab[:, None, :]
    return jnp.concatenate(
        [
            front_half * cos_part - back_half * sin_part,
            back_half * cos_part + front_half * sin_part,
        ],
        axis=-1,
    )


def rms_scale(stream):
    return lax.rsqrt(jnp.mean(stream * stream, axis=-1, keepdims=True) + EPSILON)


def matmul(left, right):
    return jnp.dot(left, right, preferred_element_type=jnp.float32)


def inner_rows(left, right):
    return lax.dot_general(
        left, right, (((0,), (0,)), ((), ())), preferred_element_type=jnp.float32
    )


def times_transposed(left, right):
    return lax.dot_general(
        left, right, (((1,), (1,)), ((), ())), preferred_element_type=jnp.float32
    )


def attend(queries, keys_rot, values_in, allowed):
    rows_here = queries.shape[0]
    kv_heads = keys_rot.shape[1]
    grouped = queries.reshape(rows_here, kv_heads, queries.shape[1] // kv_heads, HD)
    scores = jnp.einsum(
        "qkgd,skd->kgqs", grouped, keys_rot, preferred_element_type=jnp.float32
    ) * HD ** (-0.5)
    scores = jnp.where(allowed[None, None], scores, NEG_FILL)
    row_top = jnp.max(scores, axis=-1, keepdims=True)
    log_total = row_top + jnp.log(jnp.sum(jnp.exp(scores - row_top), axis=-1, keepdims=True))
    attn_probs = jnp.where(allowed[None, None], jnp.exp(scores - log_total), 0.0)
    probs_low = attn_probs.astype(jnp.bfloat16)
    attn_mixed = jnp.einsum(
        "kgqs,skd->qkgd", probs_low, values_in, preferred_element_type=jnp.float32
    )
    return (attn_probs, attn_mixed.reshape(rows_here, queries.shape[1] * HD).astype(jnp.bfloat16))


def attend_back(queries, keys_rot, values_in, attn_probs, attn_mixed, grad_mixed):
    rows_here = queries.shape[0]
    kv_heads = keys_rot.shape[1]
    groups = queries.shape[1] // kv_heads
    grouped = queries.reshape(rows_here, kv_heads, groups, HD)
    grad_grouped = grad_mixed.reshape(rows_here, kv_heads, groups, HD)
    mixed_grouped = attn_mixed.reshape(rows_here, kv_heads, groups, HD)
    delta = jnp.sum(grad_grouped.astype(jnp.float32) * mixed_grouped.astype(jnp.float32), axis=-1)
    delta = jnp.transpose(delta, (1, 2, 0))[..., None]
    grad_probs = jnp.einsum(
        "qkgd,skd->kgqs", grad_grouped, values_in, preferred_element_type=jnp.float32
    )
    grad_score = (attn_probs * (grad_probs - delta) * HD ** (-0.5)).astype(jnp.bfloat16)
    probs_low = attn_probs.astype(jnp.bfloat16)
    grad_q = jnp.einsum(
        "kgqs,skd->qkgd", grad_score, keys_rot, preferred_element_type=jnp.float32
    ).reshape(rows_here, queries.shape[1], HD)
    grad_k = jnp.einsum("kgqs,qkgd->skd", grad_score, grouped, preferred_element_type=jnp.float32)
    grad_v = jnp.einsum(
        "kgqs,qkgd->skd", probs_low, grad_grouped, preferred_element_type=jnp.float32
    )
    return (grad_q, grad_k, grad_v)


def by_blocks(array_in, count):
    return array_in.reshape((count, array_in.shape[0] // count) + array_in.shape[1:])


def from_blocks(array_in):
    return array_in.reshape((array_in.shape[0] * array_in.shape[1],) + array_in.shape[2:])


def attend_blocks(queries, keys_rot, values_in, allowed):
    count = allowed.shape[0]
    attn_probs, attn_mixed = jax.vmap(attend)(
        by_blocks(queries, count), by_blocks(keys_rot, count), by_blocks(values_in, count), allowed
    )
    return (attn_probs, from_blocks(attn_mixed))


def attend_back_blocks(queries, keys_rot, values_in, attn_probs, attn_mixed, grad_mixed):
    count = attn_probs.shape[0]
    grad_q, grad_k, grad_v = jax.vmap(attend_back)(
        by_blocks(queries, count),
        by_blocks(keys_rot, count),
        by_blocks(values_in, count),
        attn_probs,
        by_blocks(attn_mixed, count),
        by_blocks(grad_mixed, count),
    )
    return (from_blocks(grad_q), from_blocks(grad_k), from_blocks(grad_v))


def layer_forward(stream, weights, allowed, cosine, sine_tab, spread, settle):
    attn_gain, w_query, w_key, w_value, w_out, mlp_gain, w_gate, w_up, w_down = weights
    scale_one = rms_scale(stream)
    normed_one = stream * scale_one
    attn_in = spread((normed_one * attn_gain.astype(jnp.float32)).astype(jnp.bfloat16))
    rows_here = attn_in.shape[0]
    queries = rotate(
        matmul(attn_in, w_query).reshape(rows_here, w_query.shape[1] // HD, HD),
        cosine,
        sine_tab,
        1.0,
    ).astype(jnp.bfloat16)
    keys_rot = rotate(
        matmul(attn_in, w_key).reshape(rows_here, w_key.shape[1] // HD, HD), cosine, sine_tab, 1.0
    ).astype(jnp.bfloat16)
    values_in = (
        matmul(attn_in, w_value).reshape(rows_here, w_value.shape[1] // HD, HD).astype(jnp.bfloat16)
    )
    attn_probs, attn_mixed = attend_blocks(queries, keys_rot, values_in, allowed)
    middle = stream + settle(matmul(attn_mixed, w_out))
    scale_two = rms_scale(middle)
    normed_two = middle * scale_two
    mlp_in = spread((normed_two * mlp_gain.astype(jnp.float32)).astype(jnp.bfloat16))
    gate_act = matmul(mlp_in, w_gate)
    up_act = matmul(mlp_in, w_up)
    hidden = (jax.nn.silu(gate_act) * up_act).astype(jnp.bfloat16)
    result = middle + settle(matmul(hidden, w_down))
    kept_state = (
        scale_one,
        normed_one,
        attn_in,
        queries,
        keys_rot,
        values_in,
        attn_probs,
        attn_mixed,
        scale_two,
        normed_two,
        mlp_in,
        gate_act,
        up_act,
        hidden,
    )
    return (result, kept_state)


def layer_backward(stream, weights, allowed, cosine, sine_tab, grad_stream, spread, settle):
    attn_gain, w_query, w_key, w_value, w_out, mlp_gain, w_gate, w_up, w_down = weights
    _, kept_state = layer_forward(stream, weights, allowed, cosine, sine_tab, spread, settle)
    (
        scale_one,
        normed_one,
        attn_in,
        queries,
        keys_rot,
        values_in,
        attn_probs,
        attn_mixed,
        scale_two,
        normed_two,
        mlp_in,
        gate_act,
        up_act,
        hidden,
    ) = kept_state
    rows_here = attn_in.shape[0]
    grad_low = spread(grad_stream.astype(jnp.bfloat16))
    grad_down = inner_rows(hidden, grad_low)
    grad_hidden = times_transposed(grad_low, w_down)
    sigmoid_gate = jax.nn.sigmoid(gate_act)
    grad_up_act = (grad_hidden * gate_act * sigmoid_gate).astype(jnp.bfloat16)
    grad_gate_act = (
        grad_hidden * up_act * sigmoid_gate * (1.0 + gate_act * (1.0 - sigmoid_gate))
    ).astype(jnp.bfloat16)
    grad_gate = inner_rows(mlp_in, grad_gate_act)
    grad_up = inner_rows(mlp_in, grad_up_act)
    grad_mlp_in = settle(
        times_transposed(grad_gate_act, w_gate) + times_transposed(grad_up_act, w_up)
    )
    grad_mlp_gain = jnp.sum(grad_mlp_in * normed_two, axis=0)
    grad_normed = grad_mlp_in * mlp_gain.astype(jnp.float32)
    grad_middle = grad_stream + scale_two * (
        grad_normed - normed_two * jnp.mean(grad_normed * normed_two, axis=-1, keepdims=True)
    )
    grad_middle_low = spread(grad_middle.astype(jnp.bfloat16))
    grad_out = inner_rows(attn_mixed, grad_middle_low)
    grad_mixed = times_transposed(grad_middle_low, w_out).astype(jnp.bfloat16)
    grad_q, grad_k, grad_v = attend_back_blocks(
        queries, keys_rot, values_in, attn_probs, attn_mixed, grad_mixed
    )
    grad_q = (
        rotate(grad_q, cosine, sine_tab, -1.0)
        .reshape(rows_here, w_query.shape[1])
        .astype(jnp.bfloat16)
    )
    grad_k = (
        rotate(grad_k, cosine, sine_tab, -1.0)
        .reshape(rows_here, w_key.shape[1])
        .astype(jnp.bfloat16)
    )
    grad_v = grad_v.reshape(rows_here, w_value.shape[1]).astype(jnp.bfloat16)
    grad_query = inner_rows(attn_in, grad_q)
    grad_key = inner_rows(attn_in, grad_k)
    grad_value = inner_rows(attn_in, grad_v)
    grad_attn_in = settle(
        times_transposed(grad_q, w_query)
        + times_transposed(grad_k, w_key)
        + times_transposed(grad_v, w_value)
    )
    grad_attn_gain = jnp.sum(grad_attn_in * normed_one, axis=0)
    grad_normed_one = grad_attn_in * attn_gain.astype(jnp.float32)
    grad_input = grad_middle + scale_one * (
        grad_normed_one
        - normed_one * jnp.mean(grad_normed_one * normed_one, axis=-1, keepdims=True)
    )
    return (
        grad_input,
        (
            grad_attn_gain,
            grad_query,
            grad_key,
            grad_value,
            grad_out,
            grad_mlp_gain,
            grad_gate,
            grad_up,
            grad_down,
        ),
    )


def fetch_fsdp(shards, layer_idx):
    return (
        lax.all_gather(shards[1][layer_idx], "fsdp", axis=0, tiled=True),
        lax.all_gather(shards[2][layer_idx], "fsdp", axis=0, tiled=True),
        lax.all_gather(shards[3][layer_idx], "fsdp", axis=0, tiled=True),
        lax.all_gather(shards[4][layer_idx], "fsdp", axis=1, tiled=True),
        lax.all_gather(shards[6][layer_idx], "fsdp", axis=0, tiled=True),
        lax.all_gather(shards[7][layer_idx], "fsdp", axis=0, tiled=True),
        lax.all_gather(shards[8][layer_idx], "fsdp", axis=1, tiled=True),
        lax.all_gather(shards[0][layer_idx], "fsdp", axis=0, tiled=True),
        lax.all_gather(shards[5][layer_idx], "fsdp", axis=0, tiled=True),
    )


def fetch_fsdp_back(shards, layer_idx):
    return (
        lax.all_gather(shards[1][layer_idx], "fsdp", axis=0, tiled=True),
        lax.all_gather(shards[2][layer_idx], "fsdp", axis=0, tiled=True),
        lax.all_gather(shards[3][layer_idx], "fsdp", axis=0, tiled=True),
        lax.all_gather(shards[4][layer_idx], "fsdp", axis=1, tiled=True),
        lax.all_gather(shards[6][layer_idx], "fsdp", axis=0, tiled=True),
        lax.all_gather(shards[7][layer_idx], "fsdp", axis=0, tiled=True),
        lax.all_gather(shards[8][layer_idx], "fsdp", axis=1, tiled=True),
        lax.all_gather(shards[0][layer_idx], "fsdp", axis=0, tiled=True),
        lax.all_gather(shards[5][layer_idx], "fsdp", axis=0, tiled=True),
    )


def arrange(matrices, pieces):
    return (
        pieces[7],
        matrices[0],
        matrices[1],
        matrices[2],
        matrices[3],
        pieces[8],
        matrices[4],
        matrices[5],
        matrices[6],
    )


def body(
    tokens,
    lengths,
    cotangent,
    attn_gain,
    w_query,
    w_key,
    w_value,
    w_out,
    mlp_gain,
    w_gate,
    w_up,
    w_down,
):
    shards = (attn_gain, w_query, w_key, w_value, w_out, mlp_gain, w_gate, w_up, w_down)

    def spread(rows_in):
        return lax.all_gather(rows_in, "dp", axis=0, tiled=True)

    def settle(terms_in):
        return lax.psum_scatter(
            terms_in.astype(jnp.bfloat16), "dp", scatter_dimension=0, tiled=True
        ).astype(jnp.float32)

    allowed, cosine, sine_tab = jax.vmap(partial(layout, rows_here=tokens.shape[0]))(lengths)
    cosine = from_blocks(cosine)
    sine_tab = from_blocks(sine_tab)
    stream = tokens.astype(jnp.float32)
    weights_kept = []
    layer_idx = 0
    pieces = fetch_fsdp(shards, layer_idx)
    weights = arrange(pieces[:7], pieces)
    weights_kept.append(weights)
    inputs_kept = [stream]
    stream, _ = layer_forward(stream, weights, allowed, cosine, sine_tab, spread, settle)
    output = stream.astype(jnp.bfloat16)
    grad_stream = cotangent.astype(jnp.float32)
    grads_by_layer = [None] * LAYERS
    for layer_idx in reversed(range(LAYERS)):
        weights = weights_kept[layer_idx]
        grad_stream, terms = layer_backward(
            inputs_kept[layer_idx], weights, allowed, cosine, sine_tab, grad_stream, spread, settle
        )
        gains = lax.psum((terms[0], terms[5]), "dp")
        owned = (
            lax.psum_scatter(
                terms[1].astype(jnp.bfloat16), "fsdp", scatter_dimension=0, tiled=True
            ).astype(jnp.float32),
            lax.psum_scatter(
                terms[2].astype(jnp.bfloat16), "fsdp", scatter_dimension=0, tiled=True
            ).astype(jnp.float32),
            lax.psum_scatter(
                terms[3].astype(jnp.bfloat16), "fsdp", scatter_dimension=0, tiled=True
            ).astype(jnp.float32),
            lax.psum_scatter(
                terms[4].astype(jnp.bfloat16), "fsdp", scatter_dimension=1, tiled=True
            ).astype(jnp.float32),
            lax.psum_scatter(
                terms[6].astype(jnp.bfloat16), "fsdp", scatter_dimension=0, tiled=True
            ).astype(jnp.float32),
            lax.psum_scatter(
                terms[7].astype(jnp.bfloat16), "fsdp", scatter_dimension=0, tiled=True
            ).astype(jnp.float32),
            lax.psum_scatter(
                terms[8].astype(jnp.bfloat16), "fsdp", scatter_dimension=1, tiled=True
            ).astype(jnp.float32),
            lax.psum_scatter(
                gains[0].astype(jnp.bfloat16), "fsdp", scatter_dimension=0, tiled=True
            ).astype(jnp.float32),
            lax.psum_scatter(
                gains[1].astype(jnp.bfloat16), "fsdp", scatter_dimension=0, tiled=True
            ).astype(jnp.float32),
        )
        grads_by_layer[layer_idx] = arrange(owned, owned)
    stacked = tuple((jnp.stack([grads_by_layer[0][slot_idx]]) for slot_idx in range(9)))
    return (output, grad_stream) + stacked


def solution(mesh):
    placed = (
        P(("fsdp", "dp"), None),
        P("fsdp", None),
        P(("fsdp", "dp"), None),
        P(None, "fsdp"),
        P(None, "fsdp", "dp"),
        P(None, "fsdp", "dp"),
        P(None, "fsdp", "dp"),
        P(None, "dp", "fsdp"),
        P(None, "fsdp"),
        P(None, "fsdp", "dp"),
        P(None, "fsdp", "dp"),
        P(None, "dp", "fsdp"),
    )
    return jax.shard_map(
        body,
        mesh=mesh,
        in_specs=placed,
        out_specs=(
            P(("fsdp", "dp"), None),
            P(("fsdp", "dp"), None),
            P(None, "fsdp"),
            P(None, "fsdp", "dp"),
            P(None, "fsdp", "dp"),
            P(None, "fsdp", "dp"),
            P(None, "dp", "fsdp"),
            P(None, "fsdp"),
            P(None, "fsdp", "dp"),
            P(None, "fsdp", "dp"),
            P(None, "dp", "fsdp"),
        ),
        check_vma=False,
    )
```

profile of v0, /device:TPU:0, one launch (start us, length us, event | category | flops | bytes accessed | tf_op | source)
XLA Modules:
  0.0 808.7 jit_solution(16388538002550053874)
XLA Ops:
  12.3 16.0 %all-reduce.6 = (bf16[1536]{0:T(1024)(128)(2,1)S(1)}, bf16[1536]{0:T(1024)(128)(2,1)}) all-reduce(bf16[1536]{0:T(1024)(128)(2,1)S(1)} %dynamic-update-slice, bf16[1536]{0:T(1024)(128)(2,1)S(1)} %dynamic-update-slice.1), channel_id=2, replica_groups=mesh['fsdp'=8,'dp'=4] {'fsdp'}, use_global_device_ids=true, to_apply=%add | all-reduce | flops 3072 | bytes 12288
  32.4 9.4 %all-gather.2 = bf16[1,1536,192]{2,1,0:T(8,128)(2,1)S(1)} all-gather(bf16[1,192,192]{2,1,0:T(8,128)(2,1)S(1)} %copy-done.29), channel_id=4, replica_groups=mesh['fsdp'=8,'dp'=4] {'fsdp'}, dimensions={1}, use_global_device_ids=true | all-gather | bytes 663552 | tf_op jit(solution)/shard_map/all_gather | solution.py:269
  41.8 10.3 %all-gather.1 = bf16[1,1536,192]{2,1,0:T(8,128)(2,1)S(1)} all-gather(bf16[1,192,192]{2,1,0:T(8,128)(2,1)S(1)} %copy-done.30), channel_id=3, replica_groups=mesh['fsdp'=8,'dp'=4] {'fsdp'}, dimensions={1}, use_global_device_ids=true | all-gather | bytes 663552 | tf_op jit(solution)/shard_map/all_gather | solution.py:270
  53.3 13.6 %all-gather.19.cloned.1.call-done = bf16[512,1536]{1,0:T(8,128)(2,1)} async-done(((bf16[128,1536]{1,0:T(8,128)(2,1)}), bf16[512,1536]{1,0:T(8,128)(2,1)}) %all-gather.19.cloned.1.call-update) | async-done | bytes 1572880 | tf_op jit(solution)/shard_map/all_gather | solution.py:325
  71.4 20.2 %all-gather.27.cloned.1.call-done = bf16[1,1536,384]{2,1,0:T(8,128)(2,1)} async-done(((bf16[1,192,384]{2,1,0:T(8,128)(2,1)}), bf16[1,1536,384]{2,1,0:T(8,128)(2,1)}) %all-gather.27.cloned.1.call-update) | async-done | bytes 1179664 | tf_op jit(solution)/shard_map/all_gather | solution.py:268
  96.5 20.8 %all-gather.29.cloned.1.call-done = bf16[1,384,1536]{1,2,0:T(8,128)(2,1)} async-done(((bf16[1,384,192]{1,2,0:T(8,128)(2,1)}), bf16[1,384,1536]{1,2,0:T(8,128)(2,1)}) %all-gather.29.cloned.1.call-update) | async-done | bytes 1179664 | tf_op jit(solution)/shard_map/all_gather | solution.py:271
  121.5 34.9 %reduce-scatter.12.cloned.1.call-done = bf16[128,1536]{1,0:T(8,128)(2,1)} async-done(((bf16[512,1536]{1,0:T(8,128)(2,1)}), bf16[128,1536]{1,0:T(8,128)(2,1)}) %reduce-scatter.12.cloned.1.call-update) | async-done | bytes 393232 | tf_op jit(solution)/shard_map/reduce_scatter | solution.py:328
  162.1 27.2 %all-gather.33.cloned.1.call-done = bf16[1,1536,1024]{2,1,0:T(8,128)(2,1)} async-done(((bf16[1,192,1024]{2,1,0:T(8,128)(2,1)}), bf16[1,1536,1024]{2,1,0:T(8,128)(2,1)}) %all-gather.33.cloned.1.call-update) | async-done | bytes 3145744 | tf_op jit(solution)/shard_map/all_gather | solution.py:273
  189.3 39.1 %all-gather.21.cloned.1.call-done = bf16[512,1536]{1,0:T(8,128)(2,1)} async-done(((bf16[128,1536]{1,0:T(8,128)(2,1)}), bf16[512,1536]{1,0:T(8,128)(2,1)}) %all-gather.21.cloned.1.call-update) | async-done | bytes 1572880 | tf_op jit(solution)/shard_map/all_gather | solution.py:325
  233.9 27.4 %all-gather.31.cloned.1.call-done = bf16[1,1536,1024]{2,1,0:T(8,128)(2,1)} async-done(((bf16[1,192,1024]{2,1,0:T(8,128)(2,1)}), bf16[1,1536,1024]{2,1,0:T(8,128)(2,1)}) %all-gather.31.cloned.1.call-update) | async-done | bytes 3145744 | tf_op jit(solution)/shard_map/all_gather | solution.py:272
  266.8 33.1 %all-gather.23.cloned.1.call-done = bf16[512,1536]{1,0:T(8,128)(2,1)} async-done(((bf16[128,1536]{1,0:T(8,128)(2,1)}), bf16[512,1536]{1,0:T(8,128)(2,1)}) %all-gather.23.cloned.1.call-update) | async-done | bytes 1572880 | tf_op jit(solution)/shard_map/all_gather | solution.py:325
  299.9 33.0 %all-gather.35.cloned.1.call-done = bf16[1,1024,1536]{1,2,0:T(8,128)(2,1)} async-done(((bf16[1,1024,192]{1,2,0:T(8,128)(2,1)}), bf16[1,1024,1536]{1,2,0:T(8,128)(2,1)}) %all-gather.35.cloned.1.call-update) | async-done | bytes 3145744 | tf_op jit(solution)/shard_map/all_gather | solution.py:274
  345.8 35.5 %reduce-scatter.16.cloned.1.call-done = bf16[128,1536]{1,0:T(8,128)(2,1)} async-done(((bf16[512,1536]{1,0:T(8,128)(2,1)}), bf16[128,1536]{1,0:T(8,128)(2,1)}) %reduce-scatter.16.cloned.1.call-update) | async-done | bytes 393232 | tf_op jit(solution)/shard_map/reduce_scatter | solution.py:328
  402.0 19.7 %all-gather.25.cloned.1.call-done = bf16[512,1536]{1,0:T(8,128)(2,1)} async-done(((bf16[128,1536]{1,0:T(8,128)(2,1)}), bf16[512,1536]{1,0:T(8,128)(2,1)}) %all-gather.25.cloned.1.call-update) | async-done | bytes 1572880 | tf_op jit(solution)/shard_map/all_gather | solution.py:325
  458.3 11.5 %reduce-scatter.32.cloned.1.call-done = bf16[1024,192]{0,1:T(8,128)(2,1)} async-done(((bf16[1024,1536]{0,1:T(8,128)(2,1)}), bf16[1024,192]{0,1:T(8,128)(2,1)}) %reduce-scatter.32.cloned.1.call-update) | async-done | bytes 393232 | tf_op jit(solution)/shard_map/reduce_scatter | solution.py:371
  471.8 47.6 %reduce-scatter.30.cloned.1.call-done = bf16[192,1024]{1,0:T(8,128)(2,1)} async-done(((bf16[1536,1024]{1,0:T(8,128)(2,1)}), bf16[192,1024]{1,0:T(8,128)(2,1)}) %reduce-scatter.30.cloned.1.call-update) | async-done | bytes 393232 | tf_op jit(solution)/shard_map/reduce_scatter | solution.py:368
  521.3 47.3 %reduce-scatter.28.cloned.1.call-done = bf16[192,1024]{1,0:T(8,128)(2,1)} async-done(((bf16[1536,1024]{1,0:T(8,128)(2,1)}), bf16[192,1024]{1,0:T(8,128)(2,1)}) %reduce-scatter.28.cloned.1.call-update) | async-done | bytes 393232 | tf_op jit(solution)/shard_map/reduce_scatter | solution.py:365
  570.6 36.0 %reduce-scatter.24.cloned.1.call-done = bf16[192,192]{1,0:T(8,128)(2,1)} async-done(((bf16[1536,192]{1,0:T(8,128)(2,1)}), bf16[192,192]{1,0:T(8,128)(2,1)}) %reduce-scatter.24.cloned.1.call-update) | async-done | bytes 73744 | tf_op jit(solution)/shard_map/reduce_scatter | solution.py:359
  608.2 37.0 %reduce-scatter.22.cloned.1.call-done = bf16[192,192]{1,0:T(8,128)(2,1)} async-done(((bf16[1536,192]{1,0:T(8,128)(2,1)}), bf16[192,192]{1,0:T(8,128)(2,1)}) %reduce-scatter.22.cloned.1.call-update) | async-done | bytes 73744 | tf_op jit(solution)/shard_map/reduce_scatter | solution.py:356
  646.7 38.2 %reduce-scatter.26.cloned.1.call-done = bf16[384,192]{0,1:T(8,128)(2,1)} async-done(((bf16[384,1536]{0,1:T(8,128)(2,1)}), bf16[384,192]{0,1:T(8,128)(2,1)}) %reduce-scatter.26.cloned.1.call-update) | async-done | bytes 147472 | tf_op jit(solution)/shard_map/reduce_scatter | solution.py:362
  686.6 38.2 %reduce-scatter.20.cloned.1.call-done = bf16[192,384]{1,0:T(8,128)(2,1)} async-done(((bf16[1536,384]{1,0:T(8,128)(2,1)}), bf16[192,384]{1,0:T(8,128)(2,1)}) %reduce-scatter.20.cloned.1.call-update) | async-done | bytes 147472 | tf_op jit(solution)/shard_map/reduce_scatter | solution.py:353
  726.4 36.1 %reduce-scatter.18.cloned.1.call-done = bf16[128,1536]{1,0:T(8,128)(2,1)} async-done(((bf16[512,1536]{1,0:T(8,128)(2,1)}), bf16[128,1536]{1,0:T(8,128)(2,1)}) %reduce-scatter.18.cloned.1.call-update) | async-done | bytes 393232 | tf_op jit(solution)/shard_map/reduce_scatter | solution.py:328
  763.8 17.3 %all-reduce.4 = (bf16[1536]{0:T(1024)(128)(2,1)S(1)}, bf16[1536]{0:T(1024)(128)(2,1)S(1)}) all-reduce(f32[1536]{0:T(1024)S(1)} %get-tuple-element.13, f32[1536]{0:T(1024)S(1)} %copy-done.31), channel_id=1, replica_groups=mesh['fsdp'=8,'dp'=4] {'dp'}, use_global_device_ids=true, to_apply=%region_15.16 | all-reduce | flops 3072 | bytes 18432 | tf_op jit(solution)/shard_map/psum | solution.py:351
  781.1 12.5 %all-reduce.5 = (bf16[1536]{0:T(1024)(128)(2,1)S(1)}, bf16[1536]{0:T(1024)(128)(2,1)S(1)}) all-reduce(bf16[1536]{0:T(1024)(128)(2,1)S(1)} %get-tuple-element.15, bf16[1536]{0:T(1024)(128)(2,1)S(1)} %get-tuple-element.16), channel_id=15, replica_groups=mesh['fsdp'=8,'dp'=4] {'fsdp'}, use_global_device_ids=true, to_apply=%region_16.17.clone | all-reduce | flops 3072 | bytes 12288
  (219 shorter events, 130.7 us)
Async XLA Ops:
  7.2 59.6 %all-gather.19.cloned.1.call-start = ((), (), s32[]{:S(2)}) async-start(), calls=%async_computation.11 | async-start | bytes 1966080 | tf_op jit(solution)/shard_map/all_gather | solution.py:325
  30.3 61.2 %all-gather.27.cloned.1.call-start = ((), (), s32[]{:S(2)}) async-start(), calls=%async_computation.26 | async-start | bytes 1327104 | tf_op jit(solution)/shard_map/all_gather | solution.py:268
  31.0 86.3 %all-gather.29.cloned.1.call-start = ((), (), s32[]{:S(2)}) async-start(), calls=%async_computation.27 | async-start | bytes 1327104 | tf_op jit(solution)/shard_map/all_gather | solution.py:271
  31.8 124.7 %reduce-scatter.12.cloned.1.call-start = ((), (), s32[]{:S(2)}) async-start(), calls=%async_computation.12 | async-start | bytes 1966080 | tf_op jit(solution)/shard_map/reduce_scatter | solution.py:328
  120.9 68.4 %all-gather.33.cloned.1.call-start = ((), (), s32[]{:S(2)}) async-start(), calls=%async_computation.29 | async-start | bytes 3538944 | tf_op jit(solution)/shard_map/all_gather | solution.py:273
  121.5 106.9 %all-gather.21.cloned.1.call-start = ((), (), s32[]{:S(2)}) async-start(), calls=%async_computation.13 | async-start | bytes 1966080 | tf_op jit(solution)/shard_map/all_gather | solution.py:325
  159.6 101.7 %all-gather.31.cloned.1.call-start = ((), (), s32[]{:S(2)}) async-start(), calls=%async_computation.28 | async-start | bytes 3538944 | tf_op jit(solution)/shard_map/all_gather | solution.py:272
  160.4 139.5 %all-gather.23.cloned.1.call-start = ((), (), s32[]{:S(2)}) async-start(), calls=%async_computation.15 | async-start | bytes 1966080 | tf_op jit(solution)/shard_map/all_gather | solution.py:325
  161.1 171.8 %all-gather.35.cloned.1.call-start = ((), (), s32[]{:S(2)}) async-start(), calls=%async_computation.30 | async-start | bytes 3538944 | tf_op jit(solution)/shard_map/all_gather | solution.py:274
  161.9 219.5 %reduce-scatter.16.cloned.1.call-start = ((), (), s32[]{:S(2)}) async-start(), calls=%async_computation.16 | async-start | bytes 1966080 | tf_op jit(solution)/shard_map/reduce_scatter | solution.py:328
  345.8 75.8 %all-gather.25.cloned.1.call-start = ((), (), s32[]{:S(2)}) async-start(), calls=%async_computation.17 | async-start | bytes 1966080 | tf_op jit(solution)/shard_map/all_gather | solution.py:325
  385.6 84.2 %reduce-scatter.32.cloned.1.call-start = ((), (), s32[]{:S(2)}) async-start(), calls=%async_computation.25 | async-start | bytes 3538944 | tf_op jit(solution)/shard_map/reduce_scatter | solution.py:371
  390.9 128.4 %reduce-scatter.30.cloned.1.call-start = ((), (), s32[]{:S(2)}) async-start(), calls=%async_computation.24 | async-start | bytes 3538944 | tf_op jit(solution)/shard_map/reduce_scatter | solution.py:368
  396.4 172.2 %reduce-scatter.28.cloned.1.call-start = ((), (), s32[]{:S(2)}) async-start(), calls=%async_computation.23 | async-start | bytes 3538944 | tf_op jit(solution)/shard_map/reduce_scatter | solution.py:365
  401.9 204.7 %reduce-scatter.24.cloned.1.call-start = ((), (), s32[]{:S(2)}) async-start(), calls=%async_computation.21 | async-start | bytes 884736 | tf_op jit(solution)/shard_map/reduce_scatter | solution.py:359
  433.8 211.4 %reduce-scatter.22.cloned.1.call-start = ((), (), s32[]{:S(2)}) async-start(), calls=%async_computation.20 | async-start | bytes 884736 | tf_op jit(solution)/shard_map/reduce_scatter | solution.py:356
  437.0 247.9 %reduce-scatter.26.cloned.1.call-start = ((), (), s32[]{:S(2)}) async-start(), calls=%async_computation.22 | async-start | bytes 1327104 | tf_op jit(solution)/shard_map/reduce_scatter | solution.py:362
  440.7 284.0 %reduce-scatter.20.cloned.1.call-start = ((), (), s32[]{:S(2)}) async-start(), calls=%async_computation.19 | async-start | bytes 1327104 | tf_op jit(solution)/shard_map/reduce_scatter | solution.py:353
  446.1 316.3 %reduce-scatter.18.cloned.1.call-start = ((), (), s32[]{:S(2)}) async-start(), calls=%async_computation.18 | async-start | bytes 1966080 | tf_op jit(solution)/shard_map/reduce_scatter | solution.py:328
  451.5 347.6 %reduce-scatter.14.cloned.1.call-start = ((), (), s32[]{:S(2)}) async-start(), calls=%async_computation.14 | async-start | bytes 1966080 | tf_op jit(solution)/shard_map/reduce_scatter | solution.py:328
  521.3 277.9 %copy-start.7 = (bf16[128,1536]{1,0:T(8,128)(2,1)S(1)}, bf16[128,1536]{1,0:T(8,128)(2,1)}, u32[]{:S(2)}) copy-start(bf16[128,1536]{1,0:T(8,128)(2,1)} %param.14) | copy-start | bytes 1179652
  521.3 277.9 %copy-start.8 = (bf16[128,1536]{1,0:T(8,128)(2,1)S(1)}, bf16[128,1536]{1,0:T(8,128)(2,1)}, u32[]{:S(2)}) copy-start(bf16[128,1536]{1,0:T(8,128)(2,1)} %reduce-scatter.16.cloned.1.call-done) | copy-start | bytes 1179652
  521.3 277.9 %copy-start.33 = (f32[128]{0:T(128)S(1)}, f32[128]{0:T(128)}, u32[]{:S(2)}) copy-start(f32[128]{0:T(128)} %copy-done.32) | copy-start | bytes 1540
  521.3 277.9 %copy-start.39 = (f32[128]{0:T(128)S(1)}, f32[128]{0:T(128)}, u32[]{:S(2)}) copy-start(f32[128]{0:T(128)} %copy-done.38) | copy-start | bytes 1540
  (41 other events, 1191.2 us)
Sparse Core Ops, SparseCore 0:
  30.4 36.3 all-gather.18
  68.7 22.7 all-gather.26
  93.4 23.9 all-gather.28
  121.0 35.4 reduce-scatter.11
  158.2 31.0 all-gather.32
  191.3 37.0 all-gather.20
  230.2 31.0 all-gather.30
  262.9 37.0 all-gather.22
  301.8 31.0 all-gather.34
  345.9 35.4 reduce-scatter.15
  385.7 35.8 all-gather.24
  424.9 44.8 reduce-scatter.31
  473.2 46.0 reduce-scatter.29
  522.6 46.0 reduce-scatter.27
  571.6 34.9 reduce-scatter.23
  610.2 34.9 reduce-scatter.21
  648.2 36.6 reduce-scatter.25
  688.0 36.6 reduce-scatter.19
  727.0 35.4 reduce-scatter.17
  764.6 34.4 reduce-scatter.13
where the time goes:
time: 810 us; the launch traced here: 809 us
  waiting for transfers between devices  605 us (75%)
  matrix products  75 us (9%)
  blocking collectives  65.6 us (8%)
  other arithmetic  32.9 us (4%)
  between operations  16.2 us (2%)
  local copies, waits for them, and re-layouts  12.8 us (2%)
    reduce_scatter x4, waiting for transfers between devices, settle(): lax.psum_scatter(terms_in.astype(jnp.bfloat16), 'dp', scatter_dimension=0...  111 us
    all_gather x4, waiting for transfers between devices, spread(): return lax.all_gather(rows_in, 'dp', axis=0, tiled=True)  105 us
    reduce_scatter x1, waiting for transfers between devices, body(): lax.psum_scatter(terms[7].astype(jnp.bfloat16), 'fsdp', scatter_dimension...  47.6 us
    reduce_scatter x1, waiting for transfers between devices, body(): lax.psum_scatter(terms[6].astype(jnp.bfloat16), 'fsdp', scatter_dimension...  47.3 us
    reduce_scatter x1, waiting for transfers between devices, body(): lax.psum_scatter(terms[4].astype(jnp.bfloat16), 'fsdp', scatter_dimension...  38.2 us
    reduce_scatter x1, waiting for transfers between devices, body(): lax.psum_scatter(terms[1].astype(jnp.bfloat16), 'fsdp', scatter_dimension...  38.2 us
    reduce_scatter x1, waiting for transfers between devices, body(): lax.psum_scatter(terms[2].astype(jnp.bfloat16), 'fsdp', scatter_dimension...  37 us
    reduce_scatter x1, waiting for transfers between devices, body(): lax.psum_scatter(terms[3].astype(jnp.bfloat16), 'fsdp', scatter_dimension...  36 us
  transfers between devices with their start and end apart: 20, of which 20 were waited for; matrix products, arithmetic and copies ran while one was open for 11% of the time, Pallas kernels for 0%

commit v1 on v0

--- a/solution.py
+++ b/solution.py
@@ -9,6 +9,19 @@
 EPSILON = 1e-05
 ROPE_BASE = 100000.0
 NEG_FILL = -1e30
+
+
+def collect(x, axis, dim):
+    ways = lax.axis_size(axis)
+    up = [(d, (d + 1) % ways) for d in range(ways)]
+    down = [(d, (d - 1) % ways) for d in range(ways)]
+    earlier, later = ([x], [x])
+    for _ in range(ways // 2):
+        earlier.append(lax.ppermute(earlier[-1], axis, up))
+    for _ in range((ways - 1) // 2):
+        later.append(lax.ppermute(later[-1], axis, down))
+    line = jnp.concatenate([*earlier[::-1], *later[1:]], axis=dim)
+    return jnp.roll(line, (lax.axis_index(axis) - ways // 2) * x.shape[dim], axis=dim)
 
 
 def layout(seq_lengths, rows_here):
@@ -322,7 +335,7 @@
     shards = (attn_gain, w_query, w_key, w_value, w_out, mlp_gain, w_gate, w_up, w_down)
 
     def spread(rows_in):
-        return lax.all_gather(rows_in, "dp", axis=0, tiled=True)
+        return collect(rows_in, "dp", 0)
 
     def settle(terms_in):
         return lax.psum_scatter(

time: 810 us -> 670 us (0.83); the launches traced: 809 us -> 660 us
  waiting for transfers between devices: 605 us -> 408 us
  other arithmetic: 32.9 us -> 59.1 us
  starting transfers between devices: 1.47 us -> 22.3 us
    all_gather x4 -> x0, waiting for transfers between devices: 105 us -> none  [spread(): return lax.all_gather(rows_in, 'dp', axis=0, tiled=True)]
    ppermute x0 -> x12, waiting for transfers between devices: none -> 63.6 us  [the longest x8 49 us: collect(): earlier.append(lax.ppermute(earlier[-1], axis, up))]
    reduce_scatter x1, waiting for transfers between devices: 47.6 us -> 18.9 us  [body(): lax.psum_scatter(terms[7].astype(jnp.bfloat16), 'fsdp', scatter_dimension...]
    all_gather x1, waiting for transfers between devices: 27.4 us -> 0.01 us  [fetch_fsdp(): lax.all_gather(shards[6][layer_idx], 'fsdp', axis=0, tiled=True)]
    all_gather x1, waiting for transfers between devices: 27.2 us -> 0.01 us  [fetch_fsdp(): lax.all_gather(shards[7][layer_idx], 'fsdp', axis=0, tiled=True)]
    concatenate x0 -> x3, other arithmetic: none -> 25.5 us  [collect(): jnp.roll(line, (lax.axis_index(axis) - ways // 2) * x.shape[dim], axis=dim)]
    ppermute x0 -> x12, starting transfers between devices: none -> 21.2 us  [the longest x4 14.4 us: collect(): later.append(lax.ppermute(later[-1], axis, down))]
    all_gather x1, waiting for transfers between devices: 20.8 us -> 0.01 us  [fetch_fsdp(): lax.all_gather(shards[4][layer_idx], 'fsdp', axis=1, tiled=True)]
  transfers between devices with their start and end apart: 20 -> 28, of which waited for: 20 -> 20; matrix products, arithmetic and copies ran while one was open for 11% -> 19% of each run, Pallas kernels for 0% -> 0%
where the time goes in v1:
time: 670 us; the launch traced here: 660 us
  waiting for transfers between devices  408 us (61%)
  matrix products  73.6 us (11%)
  blocking collectives  67.4 us (10%)
  other arithmetic  59.1 us (9%)
  starting transfers between devices  22.3 us (3%)
  between operations  16.3 us (2%)
  local copies, waits for them, and re-layouts  13.2 us (2%)
    reduce_scatter x4, waiting for transfers between devices, settle(): lax.psum_scatter(terms_in.astype(jnp.bfloat16), 'dp', scatter_dimension=0...  99 us
    ppermute x8, waiting for transfers between devices, collect(): earlier.append(lax.ppermute(earlier[-1], axis, up))  49 us
    reduce_scatter x1, waiting for transfers between devices, body(): lax.psum_scatter(terms[6].astype(jnp.bfloat16), 'fsdp', scatter_dimension...  47.4 us
    reduce_scatter x1, waiting for transfers between devices, body(): lax.psum_scatter(terms[4].astype(jnp.bfloat16), 'fsdp', scatter_dimension...  38.4 us
    reduce_scatter x1, waiting for transfers between devices, body(): lax.psum_scatter(terms[1].astype(jnp.bfloat16), 'fsdp', scatter_dimension...  38.2 us
    reduce_scatter x1, waiting for transfers between devices, body(): lax.psum_scatter(terms[2].astype(jnp.bfloat16), 'fsdp', scatter_dimension...  37 us
    reduce_scatter x1, waiting for transfers between devices, body(): lax.psum_scatter(terms[3].astype(jnp.bfloat16), 'fsdp', scatter_dimension...  36.2 us
    unnamed x2, blocking collectives  27.9 us
  transfers between devices with their start and end apart: 28, of which 20 were waited for; matrix products, arithmetic and copies ran while one was open for 19% of the time, Pallas kernels for 0%

profile of v1, /device:TPU:0, one launch (start us, length us, event | category | flops | bytes accessed | tf_op | source)
XLA Modules:
  0.0 660.1 jit_solution(5735759648533153283)
XLA Ops:
  11.8 15.4 %all-reduce.6 = (bf16[1536]{0:T(1024)(128)(2,1)S(1)}, bf16[1536]{0:T(1024)(128)(2,1)S(1)}) all-reduce(bf16[1536]{0:T(1024)(128)(2,1)S(1)} %dynamic-update-slice, bf16[1536]{0:T(1024)(128)(2,1)S(1)} %dynamic-update-slice.1), channel_id=2, replica_groups=mesh['fsdp'=8,'dp'=4] {'fsdp'}, use_global_device_ids=true, to_apply=%add | all-reduce | flops 3072 | bytes 12288
  35.1 9.8 %all-gather.2 = bf16[1,1536,192]{2,1,0:T(8,128)(2,1)S(1)} all-gather(bf16[1,192,192]{2,1,0:T(8,128)(2,1)} %param.19), channel_id=4, replica_groups=mesh['fsdp'=8,'dp'=4] {'fsdp'}, dimensions={1}, use_global_device_ids=true | all-gather | bytes 663552 | tf_op jit(solution)/shard_map/all_gather | solution.py:282
  51.0 12.5 %all-gather.1 = bf16[1,1536,192]{2,1,0:T(8,128)(2,1)S(1)} all-gather(bf16[1,192,192]{2,1,0:T(8,128)(2,1)} %param.20), channel_id=3, replica_groups=mesh['fsdp'=8,'dp'=4] {'fsdp'}, dimensions={1}, use_global_device_ids=true | all-gather | bytes 663552 | tf_op jit(solution)/shard_map/all_gather | solution.py:283
  64.5 6.5 fusion.42
  85.2 39.5 %reduce-scatter.12.cloned.1.call-done = bf16[128,1536]{1,0:T(8,128)(2,1)} async-done(((bf16[512,1536]{1,0:T(8,128)(2,1)}), bf16[128,1536]{1,0:T(8,128)(2,1)}) %reduce-scatter.12.cloned.1.call-update) | async-done | bytes 393232 | tf_op jit(solution)/shard_map/reduce_scatter | solution.py:341
  141.1 7.4 %collective-permute-done.8 = bf16[128,1536]{1,0:T(8,128)(2,1)S(1)} collective-permute-done((bf16[128,1536]{1,0:T(8,128)(2,1)S(1)}, bf16[128,1536]{1,0:T(8,128)(2,1)S(1)}, u32[]{:S(2)}, u32[]{:S(2)}) %collective-permute-start.8) | collective-permute-done | bytes 393248 | tf_op jit(solution)/shard_map/ppermute | solution.py:22
  148.5 9.3 %collective-permute-done.7 = bf16[128,1536]{1,0:T(8,128)(2,1)S(1)} collective-permute-done((bf16[128,1536]{1,0:T(8,128)(2,1)}, bf16[128,1536]{1,0:T(8,128)(2,1)S(1)}, u32[]{:S(2)}, u32[]{:S(2)}) %collective-permute-start.7) | collective-permute-done | bytes 393248 | tf_op jit(solution)/shard_map/ppermute | solution.py:20
  163.8 10.0 %collective-permute-done.4 = bf16[128,1536]{1,0:T(8,128)(2,1)S(1)} collective-permute-done((bf16[128,1536]{1,0:T(8,128)(2,1)S(1)}, bf16[128,1536]{1,0:T(8,128)(2,1)S(1)}, u32[]{:S(2)}, u32[]{:S(2)}) %collective-permute-start.4) | collective-permute-done | bytes 393248 | tf_op jit(solution)/shard_map/ppermute | solution.py:20
  173.8 12.0 %fusion.28 = (bf16[512,1536]{1,0:T(8,128)(2,1)}, bf16[512,1536]{1,0:T(8,128)(2,1)}) fusion(s32[]{:T(128)S(6)} %select_n.33, bf16[128,1536]{1,0:T(8,128)(2,1)S(1)} %collective-permute-done.7, bf16[128,1536]{1,0:T(8,128)(2,1)} %collective-permute-done.6, bf16[128,1536]{1,0:T(8,128)(2,1)S(1)} %copy-done.6, bf16[128,1536]{1,0:T(8,128)(2,1)S(1)} %collective-permute-done.8, ...), kind=kLoop, calls=%fused_computation.71 | loop fusion | flops 25165824 | bytes 6291460 | tf_op jit(solution)/shard_map/jit(_roll_dynamic)/concatenate | solution.py:24
  196.9 27.1 %all-gather.23.cloned.1.call-done = bf16[1,1024,1536]{1,2,0:T(8,128)(2,1)} async-done(((bf16[1,1024,192]{1,2,0:T(8,128)(2,1)}), bf16[1,1024,1536]{1,2,0:T(8,128)(2,1)}) %all-gather.23.cloned.1.call-update) | async-done | bytes 3145744 | tf_op jit(solution)/shard_map/all_gather | solution.py:287
  224.0 7.2 %multiply_convert_fusion = (bf16[512,1024]{1,0:T(8,128)(2,1)S(1)}, bf16[512,1024]{1,0:T(8,128)(2,1)S(1)}, bf16[512,1024]{1,0:T(8,128)(2,1)}) fusion(f32[512,1024]{1,0:T(8,128)} %fusion.9, f32[512,1024]{1,0:T(8,128)} %fusion.5, bf16[512,1536]{1,0:T(8,128)(2,1)} %get-tuple-element.42, bf16[1,1024,1536]{1,2,0:T(8,128)(2,1)} %all-gather.23.cloned.1.call-done), kind=kOutput, calls=%fused_computation.57 | convolution fusion | flops 1619001344 | bytes 12058624 | tf_op jit(solution)/shard_map/dot_general | solution.py:72
  253.3 19.2 %reduce-scatter.16.cloned.1.call-done = bf16[128,1536]{1,0:T(8,128)(2,1)} async-done(((bf16[512,1536]{1,0:T(8,128)(2,1)}), bf16[128,1536]{1,0:T(8,128)(2,1)}) %reduce-scatter.16.cloned.1.call-update) | async-done | bytes 393232 | tf_op jit(solution)/shard_map/reduce_scatter | solution.py:341
  279.4 10.0 %collective-permute-done.9 = bf16[128,1536]{1,0:T(8,128)(2,1)S(1)} collective-permute-done((bf16[128,1536]{1,0:T(8,128)(2,1)S(1)}, bf16[128,1536]{1,0:T(8,128)(2,1)S(1)}, u32[]{:S(2)}, u32[]{:S(2)}) %collective-permute-start.9) | collective-permute-done | bytes 393248 | tf_op jit(solution)/shard_map/ppermute | solution.py:20
  294.6 10.1 %collective-permute-done.10 = bf16[128,1536]{1,0:T(8,128)(2,1)S(1)} collective-permute-done((bf16[128,1536]{1,0:T(8,128)(2,1)S(1)}, bf16[128,1536]{1,0:T(8,128)(2,1)S(1)}, u32[]{:S(2)}, u32[]{:S(2)}) %collective-permute-start.10) | collective-permute-done | bytes 393248 | tf_op jit(solution)/shard_map/ppermute | solution.py:20
  304.7 7.0 %fusion.21 = bf16[512,1536]{1,0:T(8,128)(2,1)S(1)} fusion(s32[]{:T(128)S(6)} %select_n.33, bf16[128,1536]{1,0:T(8,128)(2,1)S(1)} %collective-permute-done.10, bf16[128,1536]{1,0:T(8,128)(2,1)S(1)} %collective-permute-done.9, bf16[128,1536]{1,0:T(8,128)(2,1)S(1)} %fusion.103, bf16[128,1536]{1,0:T(8,128)(2,1)S(1)} %collective-permute-done.11), kind=kLoop, calls=%fused_computation.64 | loop fusion | flops 12582912 | bytes 3145732 | tf_op jit(solution)/shard_map/jit(_roll_dynamic)/concatenate | solution.py:24
  351.4 18.9 %reduce-scatter.30.cloned.1.call-done = bf16[192,1024]{1,0:T(8,128)(2,1)} async-done(((bf16[1536,1024]{1,0:T(8,128)(2,1)}), bf16[192,1024]{1,0:T(8,128)(2,1)}) %reduce-scatter.30.cloned.1.call-update) | async-done | bytes 393232 | tf_op jit(solution)/shard_map/reduce_scatter | solution.py:381
  372.3 47.4 %reduce-scatter.28.cloned.1.call-done = bf16[192,1024]{1,0:T(8,128)(2,1)} async-done(((bf16[1536,1024]{1,0:T(8,128)(2,1)}), bf16[192,1024]{1,0:T(8,128)(2,1)}) %reduce-scatter.28.cloned.1.call-update) | async-done | bytes 393232 | tf_op jit(solution)/shard_map/reduce_scatter | solution.py:378
  421.6 36.2 %reduce-scatter.24.cloned.1.call-done = bf16[192,192]{1,0:T(8,128)(2,1)} async-done(((bf16[1536,192]{1,0:T(8,128)(2,1)}), bf16[192,192]{1,0:T(8,128)(2,1)}) %reduce-scatter.24.cloned.1.call-update) | async-done | bytes 73744 | tf_op jit(solution)/shard_map/reduce_scatter | solution.py:372
  459.4 37.0 %reduce-scatter.22.cloned.1.call-done = bf16[192,192]{1,0:T(8,128)(2,1)} async-done(((bf16[1536,192]{1,0:T(8,128)(2,1)}), bf16[192,192]{1,0:T(8,128)(2,1)}) %reduce-scatter.22.cloned.1.call-update) | async-done | bytes 73744 | tf_op jit(solution)/shard_map/reduce_scatter | solution.py:369
  497.9 38.4 %reduce-scatter.26.cloned.1.call-done = bf16[384,192]{0,1:T(8,128)(2,1)} async-done(((bf16[384,1536]{0,1:T(8,128)(2,1)}), bf16[384,192]{0,1:T(8,128)(2,1)}) %reduce-scatter.26.cloned.1.call-update) | async-done | bytes 147472 | tf_op jit(solution)/shard_map/reduce_scatter | solution.py:375
  537.9 38.2 %reduce-scatter.20.cloned.1.call-done = bf16[192,384]{1,0:T(8,128)(2,1)} async-done(((bf16[1536,384]{1,0:T(8,128)(2,1)}), bf16[192,384]{1,0:T(8,128)(2,1)}) %reduce-scatter.20.cloned.1.call-update) | async-done | bytes 147472 | tf_op jit(solution)/shard_map/reduce_scatter | solution.py:366
  577.7 36.0 %reduce-scatter.18.cloned.1.call-done = bf16[128,1536]{1,0:T(8,128)(2,1)} async-done(((bf16[512,1536]{1,0:T(8,128)(2,1)}), bf16[128,1536]{1,0:T(8,128)(2,1)}) %reduce-scatter.18.cloned.1.call-update) | async-done | bytes 393232 | tf_op jit(solution)/shard_map/reduce_scatter | solution.py:341
  615.1 17.3 %all-reduce.4 = (bf16[1536]{0:T(1024)(128)(2,1)S(1)}, bf16[1536]{0:T(1024)(128)(2,1)S(1)}) all-reduce(f32[1536]{0:T(1024)S(1)} %get-tuple-element.14, f32[1536]{0:T(1024)S(1)} %get-tuple-element.12), channel_id=1, replica_groups=mesh['fsdp'=8,'dp'=4] {'dp'}, use_global_device_ids=true, to_apply=%region_15.17 | all-reduce | flops 3072 | bytes 18432 | tf_op jit(solution)/shard_map/psum | solution.py:364
  632.4 12.4 %all-reduce.5 = (bf16[1536]{0:T(1024)(128)(2,1)S(1)}, bf16[1536]{0:T(1024)(128)(2,1)S(1)}) all-reduce(bf16[1536]{0:T(1024)(128)(2,1)S(1)} %get-tuple-element.16, bf16[1536]{0:T(1024)(128)(2,1)S(1)} %get-tuple-element.17), channel_id=15, replica_groups=mesh['fsdp'=8,'dp'=4] {'fsdp'}, use_global_device_ids=true, to_apply=%region_16.18.clone | all-reduce | flops 3072 | bytes 12288
  (199 shorter events, 159.1 us)
Async XLA Ops:
  7.2 66.1 %all-gather.15.cloned.1.call-start = ((), (), s32[]{:S(2)}) async-start(), calls=%async_computation.22 | async-start | bytes 1327104 | tf_op jit(solution)/shard_map/all_gather | solution.py:281
  7.9 71.7 %all-gather.17.cloned.1.call-start = ((), (), s32[]{:S(2)}) async-start(), calls=%async_computation.23 | async-start | bytes 1327104 | tf_op jit(solution)/shard_map/all_gather | solution.py:284
  29.6 34.9 %collective-permute-start.2 = (bf16[128,1536]{1,0:T(8,128)(2,1)S(1)}, bf16[128,1536]{1,0:T(8,128)(2,1)S(1)}, u32[]{:S(2)}, u32[]{:S(2)}) collective-permute-start(bf16[128,1536]{1,0:T(8,128)(2,1)S(1)} %fusion.75), channel_id=1, source_target_pairs={{0,3},{1,0},{2,1},{3,2},{4,7},{5,4},{6,5},{7,6},{8,11},{9,8},{10,9... | collective-permute-start | bytes 1179656 | tf_op jit(solution)/shard_map/ppermute | solution.py:22
  33.3 15.9 %collective-permute-start = (bf16[128,1536]{1,0:T(8,128)(2,1)S(1)}, bf16[128,1536]{1,0:T(8,128)(2,1)S(1)}, u32[]{:S(2)}, u32[]{:S(2)}) collective-permute-start(bf16[128,1536]{1,0:T(8,128)(2,1)S(1)} %fusion.75), channel_id=1, source_target_pairs={{0,1},{1,2},{2,3},{3,0},{4,5},{5,6},{6,7},{7,4},{8,9},{9,10},{10,1... | collective-permute-start | bytes 1179656 | tf_op jit(solution)/shard_map/ppermute | solution.py:20
  33.3 91.4 %reduce-scatter.12.cloned.1.call-start = ((), (), s32[]{:S(2)}) async-start(), calls=%async_computation.11 | async-start | bytes 1966080 | tf_op jit(solution)/shard_map/reduce_scatter | solution.py:341
  83.3 102.5 %all-gather.21.cloned.1.call-start = ((), (), s32[]{:S(2)}) async-start(), calls=%async_computation.25 | async-start | bytes 3538944 | tf_op jit(solution)/shard_map/all_gather | solution.py:286
  83.9 107.5 %all-gather.19.cloned.1.call-start = ((), (), s32[]{:S(2)}) async-start(), calls=%async_computation.24 | async-start | bytes 3538944 | tf_op jit(solution)/shard_map/all_gather | solution.py:285
  84.4 139.6 %all-gather.23.cloned.1.call-start = ((), (), s32[]{:S(2)}) async-start(), calls=%async_computation.26 | async-start | bytes 3538944 | tf_op jit(solution)/shard_map/all_gather | solution.py:287
  85.0 187.5 %reduce-scatter.16.cloned.1.call-start = ((), (), s32[]{:S(2)}) async-start(), calls=%async_computation.13 | async-start | bytes 1966080 | tf_op jit(solution)/shard_map/reduce_scatter | solution.py:341
  85.1 45.8 %collective-permute-start.6 = (bf16[128,1536]{1,0:T(8,128)(2,1)S(1)}, bf16[128,1536]{1,0:T(8,128)(2,1)}, u32[]{:S(2)}, u32[]{:S(2)}) collective-permute-start(bf16[128,1536]{1,0:T(8,128)(2,1)S(1)} %copy-done.6), channel_id=1, source_target_pairs={{0,1},{1,2},{2,3},{3,0},{4,5},{5,6},{6,7},{7,4},{8,9},{9,10},{10,1... | collective-permute-start | bytes 1179656 | tf_op jit(solution)/shard_map/ppermute | solution.py:20
  127.6 20.9 %collective-permute-start.8 = (bf16[128,1536]{1,0:T(8,128)(2,1)S(1)}, bf16[128,1536]{1,0:T(8,128)(2,1)S(1)}, u32[]{:S(2)}, u32[]{:S(2)}) collective-permute-start(bf16[128,1536]{1,0:T(8,128)(2,1)S(1)} %copy-done.6), channel_id=1, source_target_pairs={{0,3},{1,0},{2,1},{3,2},{4,7},{5,4},{6,5},{7,6},{8,11},{9,8},{10,9... | collective-permute-start | bytes 1179656 | tf_op jit(solution)/shard_map/ppermute | solution.py:22
  130.9 26.9 %collective-permute-start.7 = (bf16[128,1536]{1,0:T(8,128)(2,1)}, bf16[128,1536]{1,0:T(8,128)(2,1)S(1)}, u32[]{:S(2)}, u32[]{:S(2)}) collective-permute-start(bf16[128,1536]{1,0:T(8,128)(2,1)} %collective-permute-done.6), channel_id=1, source_target_pairs={{0,1},{1,2},{2,3},{3,0},{4,5},{5,6},{6,7},{7,4},{8,9},{9,10},{10,1... | collective-permute-start | bytes 1179656 | tf_op jit(solution)/shard_map/ppermute | solution.py:20
  130.9 32.9 %collective-permute-start.5 = (bf16[128,1536]{1,0:T(8,128)(2,1)S(1)}, bf16[128,1536]{1,0:T(8,128)(2,1)S(1)}, u32[]{:S(2)}, u32[]{:S(2)}) collective-permute-start(bf16[128,1536]{1,0:T(8,128)(2,1)S(1)} %multiply_convert_fusion.3), channel_id=1, source_target_pairs={{0,3},{1,0},{2,1},{3,2},{4,7},{5,4},{6,5},{7,6},{8,11},{9,8},{10,9... | collective-permute-start | bytes 1179656 | tf_op jit(solution)/shard_map/ppermute | solution.py:22
  140.9 32.9 %collective-permute-start.4 = (bf16[128,1536]{1,0:T(8,128)(2,1)S(1)}, bf16[128,1536]{1,0:T(8,128)(2,1)S(1)}, u32[]{:S(2)}, u32[]{:S(2)}) collective-permute-start(bf16[128,1536]{1,0:T(8,128)(2,1)S(1)} %collective-permute-done.3), channel_id=1, source_target_pairs={{0,1},{1,2},{2,3},{3,0},{4,5},{5,6},{6,7},{7,4},{8,9},{9,10},{10,1... | collective-permute-start | bytes 1179656 | tf_op jit(solution)/shard_map/ppermute | solution.py:20
  236.9 112.5 %reduce-scatter.32.cloned.1.call-start = ((), (), s32[]{:S(2)}) async-start(), calls=%async_computation.21 | async-start | bytes 3538944 | tf_op jit(solution)/shard_map/reduce_scatter | solution.py:384
  242.6 127.8 %reduce-scatter.30.cloned.1.call-start = ((), (), s32[]{:S(2)}) async-start(), calls=%async_computation.20 | async-start | bytes 3538944 | tf_op jit(solution)/shard_map/reduce_scatter | solution.py:381
  248.0 171.6 %reduce-scatter.28.cloned.1.call-start = ((), (), s32[]{:S(2)}) async-start(), calls=%async_computation.19 | async-start | bytes 3538944 | tf_op jit(solution)/shard_map/reduce_scatter | solution.py:378
  253.3 204.5 %reduce-scatter.24.cloned.1.call-start = ((), (), s32[]{:S(2)}) async-start(), calls=%async_computation.17 | async-start | bytes 884736 | tf_op jit(solution)/shard_map/reduce_scatter | solution.py:372
  275.7 18.9 %collective-permute-start.11 = (bf16[128,1536]{1,0:T(8,128)(2,1)S(1)}, bf16[128,1536]{1,0:T(8,128)(2,1)S(1)}, u32[]{:S(2)}, u32[]{:S(2)}) collective-permute-start(bf16[128,1536]{1,0:T(8,128)(2,1)S(1)} %fusion.103), channel_id=1, source_target_pairs={{0,3},{1,0},{2,1},{3,2},{4,7},{5,4},{6,5},{7,6},{8,11},{9,8},{10,9... | collective-permute-start | bytes 1179656 | tf_op jit(solution)/shard_map/ppermute | solution.py:22
  325.4 171.0 %reduce-scatter.22.cloned.1.call-start = ((), (), s32[]{:S(2)}) async-start(), calls=%async_computation.16 | async-start | bytes 884736 | tf_op jit(solution)/shard_map/reduce_scatter | solution.py:369
  328.4 207.9 %reduce-scatter.26.cloned.1.call-start = ((), (), s32[]{:S(2)}) async-start(), calls=%async_computation.18 | async-start | bytes 1327104 | tf_op jit(solution)/shard_map/reduce_scatter | solution.py:375
  332.4 243.7 %reduce-scatter.20.cloned.1.call-start = ((), (), s32[]{:S(2)}) async-start(), calls=%async_computation.15 | async-start | bytes 1327104 | tf_op jit(solution)/shard_map/reduce_scatter | solution.py:366
  337.8 275.9 %reduce-scatter.18.cloned.1.call-start = ((), (), s32[]{:S(2)}) async-start(), calls=%async_computation.14 | async-start | bytes 1966080 | tf_op jit(solution)/shard_map/reduce_scatter | solution.py:341
  343.4 307.0 %reduce-scatter.14.cloned.1.call-start = ((), (), s32[]{:S(2)}) async-start(), calls=%async_computation.12 | async-start | bytes 1966080 | tf_op jit(solution)/shard_map/reduce_scatter | solution.py:341
  (31 other events, 869.8 us)
Sparse Core Ops, SparseCore 0:
  9.9 26.7 all-gather.14
  38.5 25.6 all-gather.16
  83.4 41.2 reduce-scatter.11
  126.4 29.6 all-gather.20
  157.9 32.1 all-gather.18
  191.8 32.1 all-gather.22
  237.1 35.4 reduce-scatter.15
  275.9 44.9 reduce-scatter.31
  324.2 46.0 reduce-scatter.29
  373.6 46.0 reduce-scatter.27
  422.8 34.9 reduce-scatter.23
  461.4 34.9 reduce-scatter.21
  499.6 36.6 reduce-scatter.25
  539.4 36.6 reduce-scatter.19
  578.2 35.4 reduce-scatter.17
  615.9 34.4 reduce-scatter.13
